TPU v7x, 32 devices: a whole 2x2x4 slice. The times are simulated.
32 devices in a mesh: gy: 8 (over y, x, core), gz: 4 (over z).
Axes of the slice: x: 2, y: 2, z: 4, core: 2. Of those that a mesh axis runs over, the one named last changes fastest.
Arguments:
- start_block: float32 [16, 64, 128, 128], P(None, 'gy', 'gz'), may hold values from -6 to 6
- diagonal: float32 [64, 128, 128], P('gy', 'gz'), may hold values from 0.25 to 4
- gaussian: float32 [512, 128], replicated, may hold values from -0.5 to 0.5
- bucket: int32 [64, 128], P('gy', 'gz'), may hold values from 0 to 3
- flip: int32 [64, 128], P('gy', 'gz'), may hold values from 0 to 1
Outputs:
- basis: float32 [16, 64, 128, 128], P(None, 'gy', 'gz')
- alphas: float32 [3, 16, 16], replicated
- factors: float32 [3, 16, 16], replicated
All inputs are finite; a program needn't handle non-finite values.
Results may differ from a plain program's by a relative error of at most 0.0003.
Values sent between devices are 32-bit elements; how exact they have to be, the bound alone decides.
No kernel may reach another device: no remote copies, remote signals or barrier semaphores. Data moves between devices by JAX's collectives and lax.ppermute only.
A program may use at most 64 MiB of HBM per device.

v0:
```python
import math

import jax
import jax.numpy as jnp
from jax import lax
from jax.sharding import PartitionSpec as P

SKETCH = 512
BUCKETS = 4
ITERS = 3


HIGH = lax.Precision.HIGHEST


def padded(value, sides, width):
    for axis, dim in sides:
        size, length = (lax.axis_size(axis), value.shape[dim])
        up = [(i, (i + 1) % size) for i in range(size - 1)]
        down = [(j, i) for i, j in up]
        last = lax.slice_in_dim(value, length - width, length, axis=dim)
        initial = lax.slice_in_dim(value, 0, width, axis=dim)
        before = lax.ppermute(last, axis, up)
        after = lax.ppermute(initial, axis, down)
        value = jnp.concatenate([before, value, after], axis=dim)
    return value


def column_weights(bucket, flip):
    labels = bucket.reshape(-1)
    signs = (1 - 2 * flip.reshape(-1)).astype(jnp.float32)
    levels = jnp.arange(BUCKETS, dtype=jnp.int32)
    return (labels[None, :] == levels[:, None]).astype(jnp.float32) * signs[None, :]


def local_sketch(block, weights, pieces):
    columns = block.reshape(block.shape[0], -1, block.shape[3])
    summed = jnp.einsum("kc,bcx->kbx", weights, columns, precision=HIGH)
    sketched = jnp.einsum("krx,kbx->bkr", pieces, summed, precision=HIGH)
    return sketched.reshape(block.shape[0], -1)


def total_sketch(partial_value, scale):
    summed = lax.psum(partial_value, ("gy", "gz"))
    return summed * scale


def apply_operator(block, diagonal):
    y_padded = padded(block, (("gy", 1),), 1)
    z_padded = padded(block, (("gz", 2),), 1)
    beside = y_padded[:, 2:] + y_padded[:, :-2] + z_padded[:, :, 2:] + z_padded[:, :, :-2]
    x_padded = jnp.pad(block, ((0, 0), (0, 0), (0, 0), (1, 1)))
    beside = beside + x_padded[..., 2:] + x_padded[..., :-2]
    return (6.0 + diagonal) * block - beside


def normalize(raw, raw_sketch):
    gram = jnp.dot(raw_sketch, raw_sketch.T, precision=HIGH)
    lower = jnp.linalg.cholesky(gram)
    identity = jnp.eye(raw.shape[0], dtype=jnp.float32)
    inverse = lax.linalg.triangular_solve(lower, identity, left_side=True, lower=True)
    basis = jnp.tensordot(inverse, raw, axes=1, precision=HIGH)
    return (basis, jnp.dot(inverse, raw_sketch, precision=HIGH), lower)


def on_device(start_block, diagonal, gaussian, bucket, flip):
    width = start_block.shape[3]
    cells = (
        width * diagonal.shape[0] * lax.axis_size("gy") * diagonal.shape[1] * lax.axis_size("gz")
    )
    scale = 1.0 / math.sqrt(cells)
    weights = column_weights(bucket, flip)
    pieces = gaussian.reshape(BUCKETS, SKETCH // BUCKETS, width)
    start_sketch = total_sketch(local_sketch(start_block, weights, pieces), scale)
    basis, sketch, lower = normalize(start_block, start_sketch)
    previous = jnp.zeros_like(basis)
    previous_sketch = jnp.zeros_like(sketch)
    alpha_list = []
    factor_list = []
    for number in range(ITERS):
        image = apply_operator(basis, diagonal)
        image_sketch = total_sketch(local_sketch(image, weights, pieces), scale)
        alpha, gamma = (
            jnp.dot(sketch, image_sketch.T, precision=HIGH),
            jnp.dot(previous_sketch, image_sketch.T, precision=HIGH),
        )
        residual = image - jnp.tensordot(alpha.T, basis, axes=1, precision=HIGH)
        residual = residual - jnp.tensordot(gamma.T, previous, axes=1, precision=HIGH)
        residual_sketch = (
            image_sketch
            - jnp.dot(alpha.T, sketch, precision=HIGH)
            - jnp.dot(gamma.T, previous_sketch, precision=HIGH)
        )
        previous, previous_sketch = (basis, sketch)
        basis, sketch, lower = normalize(residual, residual_sketch)
        alpha_list.append(alpha)
        factor_list.append(lower)
    return (basis, jnp.stack(alpha_list), jnp.stack(factor_list))


def solution(mesh):
    in_specs = (P(None, "gy", "gz", None), P("gy", "gz", None), P(), P("gy", "gz"), P("gy", "gz"))
    out_specs = (P(None, "gy", "gz", None), P(), P())
    return jax.shard_map(
        on_device, mesh=mesh, in_specs=in_specs, out_specs=out_specs, check_vma=False
    )
```

profile of v0, /device:TPU:0, one launch (start us, length us, event | category | flops | bytes accessed | tf_op | source)
XLA Modules:
  0.0 288.6 jit_solution(16151140993736077102)
XLA Ops:
  4.0 42.1 %psum.28 = f32[16,512]{1,0:T(8,128)S(1)} all-reduce(f32[16,512]{1,0:T(8,128)S(1)} %bitcast.181), channel_id=1, replica_groups=mesh['gy'=8,'gz'=4] {'gy','gz'}, use_global_device_ids=true, to_apply=%region_0.0 | all-reduce | flops 8192 | bytes 65536 | tf_op jit(solution)/shard_map/psum | solution.py:44
  46.3 1.5 cholesky.74
  50.6 2.8 fusion.24
  54.8 4.5 %collective-permute-start.3 = (f32[16,8,1,128]{3,0,2,1:T(8,128)S(1)}, f32[16,8,1,128]{3,0,2,1:T(8,128)S(1)}, u32[]{:S(2)}, u32[]{:S(2)}) collective-permute-start(f32[16,8,1,128]{3,0,2,1:T(8,128)S(1)} %get-tuple-element.22), channel_id=1, source_target_pairs={{0,1},{1,2},{2,3},{4,5},{5,6},{6,7},{8,9},{9,10},{10,11},{12,13},{... | collective-permute-start | bytes 196616 | tf_op jit(solution)/shard_map/ppermute | solution.py:23
  60.7 3.0 %collective-permute-start.1 = (f32[16,1,32,128]{3,0,2,1:T(8,128)S(1)}, f32[16,1,32,128]{3,0,2,1:T(8,128)S(1)}, u32[]{:S(2)}, u32[]{:S(2)}) collective-permute-start(f32[16,1,32,128]{3,0,2,1:T(8,128)S(1)} %get-tuple-element.20), channel_id=1, source_target_pairs={{0,4},{4,8},{8,12},{12,16},{16,20},{20,24},{24,28},{1,5},{5,9},{9,... | collective-permute-start | bytes 786440 | tf_op jit(solution)/shard_map/ppermute | solution.py:23
  64.8 1.6 fusion.2
  67.8 1.6 fusion.22
  69.9 45.5 %psum.29 = f32[16,512]{1,0:T(8,128)S(1)} all-reduce(f32[16,512]{1,0:T(8,128)S(1)} %bitcast.182), channel_id=1, replica_groups=mesh['gy'=8,'gz'=4] {'gy','gz'}, use_global_device_ids=true, to_apply=%region_3.0 | all-reduce | flops 8192 | bytes 65536 | tf_op jit(solution)/shard_map/psum | solution.py:44
  116.0 4.3 %fusion.85 = f32[16,8,32,128]{3,0,2,1:T(8,128)} fusion(f32[16,8,32,128]{3,0,2,1:T(8,128)} %copy-done.3, f32[16,16]{1,0:T(8,128)S(1)} %fusion.55), kind=kOutput, calls=%fused_computation.122 | convolution fusion | flops 100663296 | bytes 4195328 | tf_op jit(solution)/shard_map/dot_general | solution.py:87
  120.3 2.4 fusion.35
  123.1 1.5 cholesky.85
  127.3 4.7 %fusion.32 = f32[16,8,32,128]{3,0,2,1:T(8,128)S(1)} fusion(f32[16,8,32,128]{3,0,2,1:T(8,128)} %fusion.35, f32[16,8,32,128]{3,0,2,1:T(8,128)} %copy-done.8, f32[16,8,32,128]{3,0,2,1:T(8,128)} %fusion.85, f32[16,16]{1,0:T(8,128)S(1)} %fusion.60), kind=kOutput, calls=%fused_computation.50 | convolution fusion | flops 101711872 | bytes 8389632 | tf_op jit(solution)/shard_map/dot_general | solution.py:62
  133.4 3.0 %collective-permute-start.5 = (f32[16,1,32,128]{3,0,2,1:T(8,128)S(1)}, f32[16,1,32,128]{3,0,2,1:T(8,128)S(1)}, u32[]{:S(2)}, u32[]{:S(2)}) collective-permute-start(f32[16,1,32,128]{3,0,2,1:T(8,128)S(1)} %get-tuple-element.16), channel_id=1, source_target_pairs={{0,4},{4,8},{8,12},{12,16},{16,20},{20,24},{24,28},{1,5},{5,9},{9,... | collective-permute-start | bytes 786440 | tf_op jit(solution)/shard_map/ppermute | solution.py:23
  137.8 4.5 %collective-permute-start.7 = (f32[16,8,1,128]{3,0,2,1:T(8,128)S(1)}, f32[16,8,1,128]{3,0,2,1:T(8,128)S(1)}, u32[]{:S(2)}, u32[]{:S(2)}) collective-permute-start(f32[16,8,1,128]{3,0,2,1:T(8,128)S(1)} %get-tuple-element.18), channel_id=1, source_target_pairs={{0,1},{1,2},{2,3},{4,5},{5,6},{6,7},{8,9},{9,10},{10,11},{12,13},{... | collective-permute-start | bytes 196616 | tf_op jit(solution)/shard_map/ppermute | solution.py:23
  142.7 1.6 collective-permute-done.7
  144.2 1.6 fusion.5
  147.2 1.6 fusion.20
  149.3 42.0 %psum.30 = f32[16,512]{1,0:T(8,128)S(1)} all-reduce(f32[16,512]{1,0:T(8,128)S(1)} %bitcast.183), channel_id=1, replica_groups=mesh['gy'=8,'gz'=4] {'gy','gz'}, use_global_device_ids=true, to_apply=%region_4.7 | all-reduce | flops 8192 | bytes 65536 | tf_op jit(solution)/shard_map/psum | solution.py:44
  192.0 4.4 %fusion.81 = f32[16,8,32,128]{3,0,2,1:T(8,128)} fusion(f32[16,8,32,128]{3,0,2,1:T(8,128)} %copy-done.1, f32[16,16]{1,0:T(8,128)S(1)} %fusion.51), kind=kOutput, calls=%fused_computation.118 | convolution fusion | flops 100663296 | bytes 4195328 | tf_op jit(solution)/shard_map/dot_general | solution.py:87
  196.4 3.2 %fusion.79 = f32[16,8,32,128]{3,0,2,1:T(8,128)} fusion(f32[16,8,32,128]{3,0,2,1:T(8,128)S(1)} %copy-done.4, f32[16,16]{1,0:T(8,128)S(1)} %fusion.49), kind=kOutput, calls=%fused_computation.116 | convolution fusion | flops 100663296 | bytes 4195328 | tf_op jit(solution)/shard_map/dot_general | solution.py:88
  200.1 1.5 cholesky.96
  204.4 4.7 %fusion.29 = f32[16,8,32,128]{3,0,2,1:T(8,128)S(1)} fusion(f32[16,8,32,128]{3,0,2,1:T(8,128)} %fusion.79, f32[16,8,32,128]{3,0,2,1:T(8,128)} %copy-done.7, f32[16,8,32,128]{3,0,2,1:T(8,128)} %fusion.81, f32[16,16]{1,0:T(8,128)S(1)} %fusion.58), kind=kOutput, calls=%fused_computation.47 | convolution fusion | flops 101711872 | bytes 8389632 | tf_op jit(solution)/shard_map/dot_general | solution.py:62
  210.4 3.0 %collective-permute-start.9 = (f32[16,1,32,128]{3,0,2,1:T(8,128)S(1)}, f32[16,1,32,128]{3,0,2,1:T(8,128)S(1)}, u32[]{:S(2)}, u32[]{:S(2)}) collective-permute-start(f32[16,1,32,128]{3,0,2,1:T(8,128)S(1)} %get-tuple-element.12), channel_id=1, source_target_pairs={{0,4},{4,8},{8,12},{12,16},{16,20},{20,24},{24,28},{1,5},{5,9},{9,... | collective-permute-start | bytes 786440 | tf_op jit(solution)/shard_map/ppermute | solution.py:23
  214.8 4.5 %collective-permute-start.11 = (f32[16,8,1,128]{3,0,2,1:T(8,128)S(1)}, f32[16,8,1,128]{3,0,2,1:T(8,128)S(1)}, u32[]{:S(2)}, u32[]{:S(2)}) collective-permute-start(f32[16,8,1,128]{3,0,2,1:T(8,128)S(1)} %get-tuple-element.14), channel_id=1, source_target_pairs={{0,1},{1,2},{2,3},{4,5},{5,6},{6,7},{8,9},{9,10},{10,11},{12,13},{... | collective-permute-start | bytes 196616 | tf_op jit(solution)/shard_map/ppermute | solution.py:23
  219.7 1.6 collective-permute-done.11
  221.3 1.6 fusion.8
  224.2 1.6 fusion.18
  226.4 41.9 %psum.31 = f32[16,512]{1,0:T(8,128)S(1)} all-reduce(f32[16,512]{1,0:T(8,128)S(1)} %bitcast.184), channel_id=1, replica_groups=mesh['gy'=8,'gz'=4] {'gy','gz'}, use_global_device_ids=true, to_apply=%region_5.8 | all-reduce | flops 8192 | bytes 65536 | tf_op jit(solution)/shard_map/psum | solution.py:44
  268.4 4.5 %fusion.77 = f32[16,8,32,128]{3,0,2,1:T(8,128)} fusion(f32[16,8,32,128]{3,0,2,1:T(8,128)} %copy-done.5, f32[16,16]{1,0:T(8,128)S(1)} %fusion.47), kind=kOutput, calls=%fused_computation.114 | convolution fusion | flops 100663296 | bytes 4195328 | tf_op jit(solution)/shard_map/dot_general | solution.py:87
  273.3 3.2 %fusion.75 = f32[16,8,32,128]{3,0,2,1:T(8,128)} fusion(f32[16,8,32,128]{3,0,2,1:T(8,128)S(1)} %copy-done.2, f32[16,16]{1,0:T(8,128)S(1)} %fusion.45), kind=kOutput, calls=%fused_computation.112 | convolution fusion | flops 100663296 | bytes 4195328 | tf_op jit(solution)/shard_map/dot_general | solution.py:88
  281.2 4.7 %fusion.26 = f32[16,8,32,128]{3,0,2,1:T(8,128)S(1)} fusion(f32[16,16,1,1]{1,0,3,2:T(8,128)S(1)} %convolution_bitcast_fusion.4, f32[16,8,32,128]{3,0,2,1:T(8,128)} %fusion.75, f32[16,8,32,128]{3,0,2,1:T(8,128)} %copy-done.6, f32[16,8,32,128]{3,0,2,1:T(8,128)} %fusion.77), kind=kOutput, calls=%fused_computation.44 | convolution fusion | flops 101711872 | bytes 8389632 | tf_op jit(solution)/shard_map/dot_general | solution.py:62
  286.0 2.0 copy.25
  (106 shorter events, 34.8 us)
Async XLA Ops:
  0.6 1.7 copy-start
  0.6 2.8 copy-start.9
  50.6 13.1 %copy-start.10 = (f32[8,32,128]{2,1,0:T(8,128)S(1)}, f32[8,32,128]{2,1,0:T(8,128)}, u32[]{:S(2)}) copy-start(f32[8,32,128]{2,1,0:T(8,128)} %param.9) | copy-start | bytes 393220
  53.4 13.0 %copy-start.3 = (f32[16,8,32,128]{3,0,2,1:T(8,128)}, f32[16,8,32,128]{3,0,2,1:T(8,128)S(1)}, u32[]{:S(2)}) copy-start(f32[16,8,32,128]{3,0,2,1:T(8,128)S(1)} %fusion.24) | copy-start | bytes 6291460
  53.5 10.5 %collective-permute-start.2 = (f32[16,8,1,128]{3,0,2,1:T(8,128)S(1)}, f32[16,8,1,128]{3,0,2,1:T(8,128)S(1)}, u32[]{:S(2)}, u32[]{:S(2)}) collective-permute-start(f32[16,8,1,128]{3,0,2,1:T(8,128)S(1)} %get-tuple-element.21), channel_id=1, source_target_pairs={{1,0},{2,1},{3,2},{5,4},{6,5},{7,6},{9,8},{10,9},{11,10},{13,12},{... | collective-permute-start | bytes 196616 | tf_op jit(solution)/shard_map/ppermute | solution.py:24
  54.8 9.2 %collective-permute-start.3 = (f32[16,8,1,128]{3,0,2,1:T(8,128)S(1)}, f32[16,8,1,128]{3,0,2,1:T(8,128)S(1)}, u32[]{:S(2)}, u32[]{:S(2)}) collective-permute-start(f32[16,8,1,128]{3,0,2,1:T(8,128)S(1)} %get-tuple-element.22), channel_id=1, source_target_pairs={{0,1},{1,2},{2,3},{4,5},{5,6},{6,7},{8,9},{9,10},{10,11},{12,13},{... | collective-permute-start | bytes 196616 | tf_op jit(solution)/shard_map/ppermute | solution.py:23
  59.4 4.6 %collective-permute-start = (f32[16,1,32,128]{3,0,2,1:T(8,128)S(1)}, f32[16,1,32,128]{3,0,2,1:T(8,128)S(1)}, u32[]{:S(2)}, u32[]{:S(2)}) collective-permute-start(f32[16,1,32,128]{3,0,2,1:T(8,128)S(1)} %get-tuple-element.19), channel_id=1, source_target_pairs={{4,0},{8,4},{12,8},{16,12},{20,16},{24,20},{28,24},{5,1},{9,5},{13... | collective-permute-start | bytes 786440 | tf_op jit(solution)/shard_map/ppermute | solution.py:24
  60.7 4.2 %collective-permute-start.1 = (f32[16,1,32,128]{3,0,2,1:T(8,128)S(1)}, f32[16,1,32,128]{3,0,2,1:T(8,128)S(1)}, u32[]{:S(2)}, u32[]{:S(2)}) collective-permute-start(f32[16,1,32,128]{3,0,2,1:T(8,128)S(1)} %get-tuple-element.20), channel_id=1, source_target_pairs={{0,4},{4,8},{8,12},{12,16},{16,20},{20,24},{24,28},{1,5},{5,9},{9,... | collective-permute-start | bytes 786440 | tf_op jit(solution)/shard_map/ppermute | solution.py:23
  66.5 1.3 copy-start.8
  132.1 13.8 %copy-start.1 = (f32[16,8,32,128]{3,0,2,1:T(8,128)}, f32[16,8,32,128]{3,0,2,1:T(8,128)S(1)}, u32[]{:S(2)}) copy-start(f32[16,8,32,128]{3,0,2,1:T(8,128)S(1)} %fusion.32) | copy-start | bytes 6291460
  132.1 12.1 %collective-permute-start.4 = (f32[16,1,32,128]{3,0,2,1:T(8,128)S(1)}, f32[16,1,32,128]{3,0,2,1:T(8,128)S(1)}, u32[]{:S(2)}, u32[]{:S(2)}) collective-permute-start(f32[16,1,32,128]{3,0,2,1:T(8,128)S(1)} %get-tuple-element.15), channel_id=1, source_target_pairs={{4,0},{8,4},{12,8},{16,12},{20,16},{24,20},{28,24},{5,1},{9,5},{13... | collective-permute-start | bytes 786440 | tf_op jit(solution)/shard_map/ppermute | solution.py:24
  133.4 10.8 %collective-permute-start.5 = (f32[16,1,32,128]{3,0,2,1:T(8,128)S(1)}, f32[16,1,32,128]{3,0,2,1:T(8,128)S(1)}, u32[]{:S(2)}, u32[]{:S(2)}) collective-permute-start(f32[16,1,32,128]{3,0,2,1:T(8,128)S(1)} %get-tuple-element.16), channel_id=1, source_target_pairs={{0,4},{4,8},{8,12},{12,16},{16,20},{20,24},{24,28},{1,5},{5,9},{9,... | collective-permute-start | bytes 786440 | tf_op jit(solution)/shard_map/ppermute | solution.py:23
  136.5 6.2 %collective-permute-start.6 = (f32[16,8,1,128]{3,0,2,1:T(8,128)S(1)}, f32[16,8,1,128]{3,0,2,1:T(8,128)S(1)}, u32[]{:S(2)}, u32[]{:S(2)}) collective-permute-start(f32[16,8,1,128]{3,0,2,1:T(8,128)S(1)} %get-tuple-element.17), channel_id=1, source_target_pairs={{1,0},{2,1},{3,2},{5,4},{6,5},{7,6},{9,8},{10,9},{11,10},{13,12},{... | collective-permute-start | bytes 196616 | tf_op jit(solution)/shard_map/ppermute | solution.py:24
  137.8 6.4 %collective-permute-start.7 = (f32[16,8,1,128]{3,0,2,1:T(8,128)S(1)}, f32[16,8,1,128]{3,0,2,1:T(8,128)S(1)}, u32[]{:S(2)}, u32[]{:S(2)}) collective-permute-start(f32[16,8,1,128]{3,0,2,1:T(8,128)S(1)} %get-tuple-element.18), channel_id=1, source_target_pairs={{0,1},{1,2},{2,3},{4,5},{5,6},{6,7},{8,9},{9,10},{10,11},{12,13},{... | collective-permute-start | bytes 196616 | tf_op jit(solution)/shard_map/ppermute | solution.py:23
  145.9 1.3 copy-start.7
  192.0 4.5 %copy-start.4 = (f32[16,8,32,128]{3,0,2,1:T(8,128)S(1)}, f32[16,8,32,128]{3,0,2,1:T(8,128)}, u32[]{:S(2)}) copy-start(f32[16,8,32,128]{3,0,2,1:T(8,128)} %copy-done.3) | copy-start | bytes 6291460
  209.1 13.8 %copy-start.5 = (f32[16,8,32,128]{3,0,2,1:T(8,128)}, f32[16,8,32,128]{3,0,2,1:T(8,128)S(1)}, u32[]{:S(2)}) copy-start(f32[16,8,32,128]{3,0,2,1:T(8,128)S(1)} %fusion.29) | copy-start | bytes 6291460
  209.1 12.1 %collective-permute-start.8 = (f32[16,1,32,128]{3,0,2,1:T(8,128)S(1)}, f32[16,1,32,128]{3,0,2,1:T(8,128)S(1)}, u32[]{:S(2)}, u32[]{:S(2)}) collective-permute-start(f32[16,1,32,128]{3,0,2,1:T(8,128)S(1)} %get-tuple-element.11), channel_id=1, source_target_pairs={{4,0},{8,4},{12,8},{16,12},{20,16},{24,20},{28,24},{5,1},{9,5},{13... | collective-permute-start | bytes 786440 | tf_op jit(solution)/shard_map/ppermute | solution.py:24
  210.4 10.8 %collective-permute-start.9 = (f32[16,1,32,128]{3,0,2,1:T(8,128)S(1)}, f32[16,1,32,128]{3,0,2,1:T(8,128)S(1)}, u32[]{:S(2)}, u32[]{:S(2)}) collective-permute-start(f32[16,1,32,128]{3,0,2,1:T(8,128)S(1)} %get-tuple-element.12), channel_id=1, source_target_pairs={{0,4},{4,8},{8,12},{12,16},{16,20},{20,24},{24,28},{1,5},{5,9},{9,... | collective-permute-start | bytes 786440 | tf_op jit(solution)/shard_map/ppermute | solution.py:23
  213.5 6.2 %collective-permute-start.10 = (f32[16,8,1,128]{3,0,2,1:T(8,128)S(1)}, f32[16,8,1,128]{3,0,2,1:T(8,128)S(1)}, u32[]{:S(2)}, u32[]{:S(2)}) collective-permute-start(f32[16,8,1,128]{3,0,2,1:T(8,128)S(1)} %get-tuple-element.13), channel_id=1, source_target_pairs={{1,0},{2,1},{3,2},{5,4},{6,5},{7,6},{9,8},{10,9},{11,10},{13,12},{... | collective-permute-start | bytes 196616 | tf_op jit(solution)/shard_map/ppermute | solution.py:24
  214.8 6.4 %collective-permute-start.11 = (f32[16,8,1,128]{3,0,2,1:T(8,128)S(1)}, f32[16,8,1,128]{3,0,2,1:T(8,128)S(1)}, u32[]{:S(2)}, u32[]{:S(2)}) collective-permute-start(f32[16,8,1,128]{3,0,2,1:T(8,128)S(1)} %get-tuple-element.14), channel_id=1, source_target_pairs={{0,1},{1,2},{2,3},{4,5},{5,6},{6,7},{8,9},{9,10},{10,11},{12,13},{... | collective-permute-start | bytes 196616 | tf_op jit(solution)/shard_map/ppermute | solution.py:23
  222.9 1.4 copy-start.6
  268.4 4.9 %copy-start.2 = (f32[16,8,32,128]{3,0,2,1:T(8,128)S(1)}, f32[16,8,32,128]{3,0,2,1:T(8,128)}, u32[]{:S(2)}) copy-start(f32[16,8,32,128]{3,0,2,1:T(8,128)} %copy-done.1) | copy-start | bytes 6291460
where the time goes:
time: 290 us; the launch traced here: 289 us
  blocking collectives  172 us (59%)
  matrix products  51.2 us (18%)
  starting transfers between devices  30.5 us (11%)
  other arithmetic  22.3 us (8%)
  local copies, waits for them, and re-layouts  7.46 us (3%)
  waiting for transfers between devices  4.42 us (2%)
    psum x4, blocking collectives, total_sketch(): summed = lax.psum(partial_value, ('gy', 'gz'))  172 us
    ppermute x6, starting transfers between devices, padded(): before = lax.ppermute(last, axis, up)  22.8 us
    dot_general x4, matrix products, normalize(): basis = jnp.tensordot(inverse, raw, axes=1, precision=HIGH)  17 us
    dot_general x3, matrix products, on_device(): residual = image - jnp.tensordot(alpha.T, basis, axes=1, precision=HIGH)  13.3 us
    dot_general x3, matrix products, on_device(): jnp.tensordot(gamma.T, previous, axes=1, precision=HIGH)  8.81 us
    another operation x12, other arithmetic, normalize(): lower = jnp.linalg.cholesky(gram)  8.61 us
    ppermute x6, starting transfers between devices, padded(): after = lax.ppermute(initial, axis, down)  7.75 us
    dot_general x4, matrix products, local_sketch(): summed = jnp.einsum('kc,bcx->kbx', weights, columns, precision=HIGH)  5.98 us
  transfers between devices with their start and end apart: 12, of which 5 were waited for; matrix products, arithmetic and copies ran while one was open for 0% of the time, Pallas kernels for 0%

commit v1 on v0

v1 whole, which is shorter than its diff:
```python
import functools
import math

import jax
import jax.numpy as jnp
from jax import lax
from jax.experimental import pallas as pl
from jax.experimental.pallas import tpu as pltpu
from jax.sharding import PartitionSpec as P

BUCKETS = 4
ITERS = 3
CENTRE = 8.125
AXES = ("gy", "gz")
HIGH = lax.Precision.HIGHEST
VMEM = pltpu.MemorySpace.VMEM
HBM = pltpu.MemorySpace.HBM
MIB = 1 << 20


def call(body, name, outs, ins, scratch=(), limit=16):
    return pl.pallas_call(
        body,
        out_shape=[jax.ShapeDtypeStruct(shape, kind) for shape, kind, _ in outs],
        in_specs=[pl.BlockSpec(memory_space=space) for space in ins],
        out_specs=[pl.BlockSpec(memory_space=space) for _, _, space in outs],
        scratch_shapes=list(scratch),
        compiler_params=pltpu.CompilerParams(vmem_limit_bytes=limit * MIB),
        name=name,
    )


def odd(axis):
    return lax.axis_index(axis) % 2 == 1


def pairs(axis, first):
    size = lax.axis_size(axis)
    swap = {}
    for i in range(first, size - 1 + first, 2):
        swap[i % size], swap[(i + 1) % size] = (i + 1) % size, i % size
    return sorted(swap.items())


def swapped(axis, within, across):
    return lax.ppermute(within, axis, pairs(axis, 0)), lax.ppermute(across, axis, pairs(axis, 1))


def edge(axis):
    index = lax.axis_index(axis)
    return index == 0, index == lax.axis_size(axis) - 1


def when_sides(axis, act):
    @pl.when(odd(axis))
    def _():
        act(0, 1)

    @pl.when(jnp.logical_not(odd(axis)))
    def _():
        act(1, 0)


def small_y(diag, bucket, flip, code_out, within, across):
    ny, nz, _ = diag.shape
    code = (bucket[...] + 1).astype(jnp.float32) * (1 - 2 * flip[...]).astype(jnp.float32)
    code_out[...] = jnp.zeros_like(code_out)
    code_out[:, 0:nz] = code

    def pack(out, low):
        if low:
            layers, rows = diag[0:2], code_out[0:3]
        else:
            layers, rows = diag[ny - 2 : ny], code_out[ny - 3 : ny]
        out[0 : 2 * nz] = layers.reshape(2 * nz, layers.shape[2])
        out[2 * nz : 2 * nz + 8] = jnp.zeros_like(out[2 * nz : 2 * nz + 8])
        out[2 * nz : 2 * nz + 3] = rows

    def act(side_within, side_across):
        pack(within, side_within == 0)
        pack(across, side_across == 0)

    when_sides("gy", act)


def turned(v, vt, ny, nz):
    count = v.shape[0] // (ny * nz)

    def move(col, carry):
        vt[col] = v[pl.ds(col, count, stride=ny * nz), :]
        return carry

    lax.fori_loop(0, ny * nz, move, 0, unroll=16)


def pack_y(vt, after, within, across, ny, nz):
    def act(side_within, side_across):
        for out, side in ((within, side_within), (across, side_across)):
            out[...] = vt[0 : 3 * nz] if side == 0 else vt[(ny - 3) * nz : ny * nz]

    when_sides("gy", act)


def small_z(diag, code, got_within, got_across, codes_out, within, across):
    ny, nz, width = diag.shape
    codes_out[...] = jnp.zeros_like(codes_out)
    codes_out[3 : 3 + ny] = code[...]

    def gather(side_within, side_across):
        for got, side, at_edge in zip(
            (got_within, got_across), (side_within, side_across), ("w", "a")
        ):
            start = 0 if side == 0 else 3 + ny
            wrapped = edge("gy")[side]
            rows = got[2 * nz : 2 * nz + 3]
            codes_out[start : start + 3] = jnp.where(wrapped, jnp.zeros_like(rows), rows)

    when_sides("gy", gather)
    y_low_within = odd("gy")

    def pack(out, low):
        z0 = 0 if low else nz - 2
        for t in range(2):
            for y in range(ny):
                out[(y + 2) * 2 + t : (y + 2) * 2 + t + 1] = diag[y, z0 + t : z0 + t + 1]
            for layer in range(2):
                row = layer * nz + z0 + t
                a = got_within[row : row + 1]
                b = got_across[row : row + 1]
                out[layer * 2 + t : layer * 2 + t + 1] = jnp.where(y_low_within, a, b)
                high = (ny + 2 + layer) * 2 + t
                out[high : high + 1] = jnp.where(y_low_within, b, a)
        base = 2 * (ny + 4)
        c0 = 0 if low else nz - 3
        out[base : base + 16] = jnp.zeros_like(out[base : base + 16])
        out[base : base + 16, 0:3] = codes_out[:, c0 : c0 + 3]

    def act(side_within, side_across):
        pack(within, side_within == 0)
        pack(across, side_across == 0)

    when_sides("gz", act)


def spread_diagonal(dr, diag, y_within, y_across, z_within, z_across):
    ny, nz, width = diag.shape
    shift = 6.0 - CENTRE

    def put(y, z, row):
        dr[y, z] = jnp.broadcast_to(row + shift, (8, width))

    for y in range(ny):
        for z in range(nz):
            put(y + 2, z + 2, diag[y, z : z + 1])

    def y_sides(side_within, side_across):
        for got, side in ((y_within, side_within), (y_across, side_across)):
            start = 0 if side == 0 else ny + 2
            for layer in range(2):
                for z in range(nz):
                    row = layer * nz + z
                    put(start + layer, z + 2, got[row : row + 1])

    def z_sides(side_within, side_across):
        for got, side in ((z_within, side_within), (z_across, side_across)):
            start = 0 if side == 0 else nz + 2
            for y in range(ny + 4):
                for t in range(2):
                    put(y, start + t, got[2 * y + t : 2 * y + t + 1])

    when_sides("gy", y_sides)
    when_sides("gz", z_sides)


def stencil(source, target, dr, ys, zs, source_at, target_at):
    half, width = 8, source.shape[3]
    lane = lax.broadcasted_iota(jnp.int32, (half, width), 1)
    first, last = lane == 0, lane == width - 1

    def row(i, carry):
        sy, ty, dy = i + (ys[0] + source_at), i + (ys[0] + target_at), i + (ys[0] + 2)
        for z in range(zs[0], zs[1]):
            sz, tz = z + source_at, z + target_at
            weight = dr[dy, z + 2]
            for h in range(0, source.shape[2], half):
                part = pl.ds(h, half)
                here = source[sy, sz, part]
                around = source[sy - 1, sz, part] + source[sy + 1, sz, part]
                around = around + (source[sy, sz - 1, part] + source[sy, sz + 1, part])
                left = jnp.where(first, 0.0, pltpu.roll(here, 1, 1))
                right = jnp.where(last, 0.0, pltpu.roll(here, width - 1, 1))
                target[ty, tz, part] = weight * here - (around + (left + right))
        return carry

    lax.fori_loop(0, ys[1] - ys[0], row, 0)


def clear_edges(field, ny, nz, at, reach):
    y_low, y_high = edge("gy")
    z_low, z_high = edge("gz")
    for flag, y in ((y_low, -1), (y_high, ny)):

        @pl.when(flag)
        def _():
            for z in range(-reach, nz + reach):
                field[y + at, z + at] = jnp.zeros(field.shape[2:], field.dtype)

    for flag, z in ((z_low, -1), (z_high, nz)):

        @pl.when(flag)
        def _():
            for y in range(-reach, ny + reach):
                field[y + at, z + at] = jnp.zeros(field.shape[2:], field.dtype)


def weights_to_scalars(codes, z_within, z_across, table, scalars, sem, ny, nz):
    base = 2 * (ny + 4)
    z_low, z_high = edge("gz")
    low_within = odd("gz")
    a = z_within[base : base + 16]
    b = z_across[base : base + 16]
    low = jnp.where(z_low, 0.0, jnp.where(low_within, a, b))
    high = jnp.where(z_high, 0.0, jnp.where(low_within, b, a))
    lane = lax.broadcasted_iota(jnp.int32, (16, 128), 1)
    whole = jnp.where(
        lane < 3,
        low,
        jnp.where(
            lane < nz + 3,
            pltpu.roll(codes[...], 3, 1),
            jnp.where(lane < nz + 6, pltpu.roll(high, nz + 3, 1), 0.0),
        ),
    )
    sign = jnp.where(whole > 0, 1.0, -1.0)
    for k in range(BUCKETS):
        weight = jnp.where(jnp.abs(whole) == k + 1, sign, 0.0)
        table[16 * k : 16 * k + 16] = weight
        beside = pltpu.roll(weight, 1, 1) + pltpu.roll(weight, 127, 1)
        beside = beside + pltpu.roll(weight, 1, 0) + pltpu.roll(weight, 15, 0)
        at = 16 * (BUCKETS + k)
        table[at : at + 16] = beside
    copy = pltpu.make_async_copy(table, scalars, sem)
    copy.start()
    return copy


def local_sketches(
    vt, diag, code, y_within, y_across, z_within, z_across, gaussian, keep_out, give_out,
    e0, e1, e2, dr, table, scalars, sums, sem,
):
    ny, nz, width = diag.shape
    count = vt.shape[1]
    copy = weights_to_scalars(code, z_within, z_across, table, scalars, sem, ny, nz)
    spread_diagonal(dr, diag, y_within, y_across, z_within, z_across)
    e0[...] = jnp.zeros_like(e0)
    e1[...] = jnp.zeros_like(e1)
    for y in range(ny):
        e0[y + 2, 2 : 2 + nz] = vt[y * nz : (y + 1) * nz]
    copy.wait()
    blank = tuple(jnp.zeros((count, width), jnp.float32) for _ in range(BUCKETS))

    def total(field, level, at):
        def row(i, acc):
            acc = list(acc)
            for z in range(-level, nz + level):
                value = field[i + (at - level), z + at]
                for k in range(BUCKETS):
                    weight = scalars[i + (16 * k + 3 - level), z + 3]
                    acc[k] = acc[k] + weight * value
            return tuple(acc)

        acc = lax.fori_loop(0, ny + 2 * level, row, blank)
        for k in range(BUCKETS):
            sums[k, level * count : (level + 1) * count] = acc[k]
        return acc

    def applied(field, level, at):
        def row(i, acc):
            acc = list(acc)
            for z in range(-level, nz + level):
                value = field[i + (at - level), z + at]
                weight = dr[i + (2 - level), z + 2]
                for k in range(BUCKETS):
                    here = scalars[i + (16 * k + 3 - level), z + 3]
                    beside = scalars[i + (16 * (BUCKETS + k) + 3 - level), z + 3]
                    both = weight * here - beside
                    acc[k] = acc[k] + jnp.concatenate([both, both], axis=0) * value
            return tuple(acc)

        return lax.fori_loop(0, ny + 2 * level, row, blank)

    total(e0, 0, 2)
    stencil(e0, e1, dr, (-1, ny + 1), (-1, nz + 1), 2, 3)
    total(e1, 1, 3)
    clear_edges(e1, ny, nz, 3, 1)
    stencil(e1, e2, dr, (-2, ny + 2), (-2, nz + 2), 3, 2)
    last = total(e2, 2, 2)
    clear_edges(e2, ny, nz, 2, 2)
    higher = applied(e2, 2, 2)
    lane = lax.broadcasted_iota(jnp.int32, (count, width), 1)
    for k in range(BUCKETS):
        left = jnp.where(lane == 0, 0.0, pltpu.roll(last[k], 1, 1))
        right = jnp.where(lane == width - 1, 0.0, pltpu.roll(last[k], width - 1, 1))
        sums[k, 3 * count : 4 * count] = higher[k] - (left + right)
    rows = gaussian.shape[0] // BUCKETS

    def part(k):
        return lax.dot_general(
            sums[k],
            gaussian[k * rows : (k + 1) * rows],
            (((1,), (1,)), ((), ())),
            precision=HIGH,
            preferred_element_type=jnp.float32,
        )

    upper = odd("gy")
    size = (ITERS + 1) * count
    for k in range(BUCKETS // 2):
        one, two = part(k), part(k + BUCKETS // 2)
        keep_out[k * size : (k + 1) * size] = jnp.where(upper, two, one)
        give_out[k * size : (k + 1) * size] = jnp.where(upper, one, two)


def pack_z(vt, y_within, y_across, after, within, across, ny, nz):
    def act(side_within, side_across):
        for out, side in ((within, side_within), (across, side_across)):
            z0 = 0 if side == 0 else nz - 3
            for y in range(ny):
                out[y + 3] = vt[y * nz + z0 : y * nz + z0 + 3]

            def corners(low, high):
                for layer in range(3):
                    out[layer] = low[layer * nz + z0 : layer * nz + z0 + 3]
                    out[ny + 3 + layer] = high[layer * nz + z0 : layer * nz + z0 + 3]

            @pl.when(odd("gy"))
            def _():
                corners(y_within, y_across)

            @pl.when(jnp.logical_not(odd("gy")))
            def _():
                corners(y_across, y_within)

    when_sides("gz", act)


def krylov(
    vt, diag, dy_within, dy_across, dz_within, dz_across,
    y_within, y_across, z_within, z_across, high_out, low_out,
    e0, e1, dr, high, low, sems,
):
    ny, nz, width = diag.shape
    count = vt.shape[1]
    spread_diagonal(dr, diag, dy_within, dy_across, dz_within, dz_across)
    for y in range(ny):
        e0[y + 3, 3 : 3 + nz] = vt[y * nz : (y + 1) * nz]
    y_edges, z_edges = edge("gy"), edge("gz")
    blank_y = jnp.zeros((nz, count, width), jnp.float32)
    blank_z = jnp.zeros((3, count, width), jnp.float32)

    def y_sides(side_within, side_across):
        for got, side in ((y_within, side_within), (y_across, side_across)):
            start = 0 if side == 0 else ny + 3
            for layer in range(3):
                e0[start + layer, 3 : 3 + nz] = got[layer * nz : (layer + 1) * nz]

            @pl.when(y_edges[side])
            def _():
                for layer in range(3):
                    e0[start + layer, 3 : 3 + nz] = blank_y

    def z_sides(side_within, side_across):
        for got, side in ((z_within, side_within), (z_across, side_across)):
            start = 0 if side == 0 else nz + 3
            for y in range(ny + 6):
                e0[y, start : start + 3] = got[y]

            @pl.when(z_edges[side])
            def _():
                for y in range(ny + 6):
                    e0[y, start : start + 3] = blank_z

            for y_side in range(2):

                @pl.when(y_edges[y_side])
                def _():
                    for layer in range(3):
                        y = layer if y_side == 0 else ny + 3 + layer
                        e0[y, start : start + 3] = blank_z

    when_sides("gy", y_sides)
    when_sides("gz", z_sides)

    def halves(field, level):
        def row(y, carry):
            for z in range(nz):
                value = field[y + 3, z + 3]
                top = value.astype(jnp.bfloat16)
                rows = pl.ds(level * count, count)
                high[y * nz + z, rows] = top
                low[y * nz + z, rows] = (value - top.astype(jnp.float32)).astype(jnp.bfloat16)
            return carry

        lax.fori_loop(0, ny, row, 0)

    halves(e0, 0)
    stencil(e0, e1, dr, (-2, ny + 2), (-2, nz + 2), 3, 3)
    clear_edges(e1, ny, nz, 3, 2)
    halves(e1, 1)
    stencil(e1, e0, dr, (-1, ny + 1), (-1, nz + 1), 3, 3)
    clear_edges(e0, ny, nz, 3, 1)
    halves(e0, 2)
    stencil(e0, e1, dr, (0, ny), (0, nz), 3, 3)
    halves(e1, 3)
    one = pltpu.make_async_copy(high, high_out, sems.at[0])
    two = pltpu.make_async_copy(low, low_out, sems.at[1])
    one.start()
    two.start()
    one.wait()
    two.wait()


def product(a, b, axis):
    return lax.dot_general(
        a, b, (((1,), (axis,)), ((), ())), precision=HIGH, preferred_element_type=jnp.float32
    )


def factored(gram, block):
    count = gram.shape[0]
    width = 128
    columns = [jnp.broadcast_to(gram[:, j : j + 1], (count, width)) for j in range(count)]
    pieces = [block[:, c : c + width] for c in range(0, block.shape[1], width)]
    row = lax.broadcasted_iota(jnp.int32, (count, width), 0)
    lane = lax.broadcasted_iota(jnp.int32, (count, width), 1)
    lower = jnp.zeros((count, width), jnp.float32)
    scale = jnp.zeros((count, width), jnp.float32)
    for j in range(count):
        pivot = columns[j][j : j + 1]
        root = 1.0 / jnp.sqrt(pivot)
        inverse = root * root
        lower = jnp.where((lane == j) & (row >= j), columns[j] * root, lower)
        scale = jnp.where(row == j, jnp.broadcast_to(root, (count, width)), scale)
        under = jnp.where(row > j, columns[j] * inverse, 0.0)
        for m in range(j + 1, count):
            columns[m] = columns[m] - under * columns[m][j : j + 1]
        pieces = [piece - under * piece[j : j + 1] for piece in pieces]
    return lower, jnp.concatenate([piece * scale for piece in pieces], axis=1)


def finish(kept, got, high_in, low_in, out, alphas, factors, high, low, block, sems, out_sem, ny, nz, scale):
    count = alphas.shape[1]
    size = (ITERS + 1) * count
    width = kept.shape[1]
    one = pltpu.make_async_copy(high_in, high, sems.at[0])
    two = pltpu.make_async_copy(low_in, low, sems.at[1])
    one.start()
    two.start()
    upper = odd("gy")
    first = jnp.where(upper, got[...], kept[...])
    second = jnp.where(upper, kept[...], got[...])
    parts = [first[0:size], first[size:], second[0:size], second[size:]]
    whole = jnp.concatenate(parts, axis=1) * scale
    row = lax.broadcasted_iota(jnp.int32, (count, width), 0)
    lane = lax.broadcasted_iota(jnp.int32, (count, width), 1)
    identity = jnp.where(row == lane, 1.0, 0.0)
    start = whole[0:count]
    lower, current = factored(
        product(start, start, 1), jnp.concatenate([start, identity], axis=1)
    )
    previous = jnp.zeros_like(current)
    span = whole.shape[1]
    for number in range(ITERS):
        raised = pltpu.roll(current[:, span:], count, 1)
        image_sketch = product(raised[:, 0:size], whole, 0)
        image = jnp.concatenate([image_sketch, raised], axis=1) + CENTRE * current
        both = jnp.concatenate([current, previous], axis=0)
        mixed = product(image[:, 0:span], both[:, 0:span], 1)
        alphas[number] = product(current[:, 0:span], image[:, 0:span], 1)
        residual = image - product(mixed, both, 0)
        previous = current
        sketch = residual[:, 0:span]
        lower, current = factored(product(sketch, sketch, 1), residual)
        factors[number] = lower[:, 0:count]
    mix = current[:, span : span + size]
    group = 4
    tiled = jnp.concatenate([mix] * group, axis=1)
    tiled = jnp.concatenate([tiled] * group, axis=0)
    at_row = lax.broadcasted_iota(jnp.int32, tiled.shape, 0) // count
    at_lane = lax.broadcasted_iota(jnp.int32, tiled.shape, 1) // size
    tiled = jnp.where(at_row == at_lane, tiled, 0.0)
    mix_high = tiled.astype(jnp.bfloat16)
    mix_low = (tiled - mix_high.astype(jnp.float32)).astype(jnp.bfloat16)
    one.wait()
    two.wait()

    def dot(a, b):
        return jnp.dot(a, b, preferred_element_type=jnp.float32)

    def copies(y):
        return [
            pltpu.make_async_copy(block.at[y, pl.ds(b * nz, nz)], out.at[b, y], out_sem)
            for b in range(count)
        ]

    def layer(y, carry):
        for z in range(0, nz, group):
            col = y * nz + z
            top = high[pl.ds(col, group)].reshape(group * size, width)
            bottom = low[pl.ds(col, group)].reshape(group * size, width)
            value = dot(mix_high, top) + (dot(mix_high, bottom) + dot(mix_low, top))
            for c in range(group):
                block[y, pl.ds(z + c, count, stride=nz), :] = value[c * count : (c + 1) * count]
        for copy in copies(y):
            copy.start()
        return carry

    lax.fori_loop(0, ny, layer, 0)

    def drain(y, carry):
        for copy in copies(y):
            copy.wait()
        return carry

    lax.fori_loop(0, ny, drain, 0)


def reduced(kept, given):
    ny, nz = lax.axis_size("gy"), lax.axis_size("gz")
    total = ny * nz

    def exchange(value, bit):
        return lax.ppermute(value, AXES, [(i, i ^ bit) for i in range(total)])

    half = kept + exchange(given, nz)
    bit = 1
    while bit < nz:
        half = half + exchange(half, bit)
        bit *= 2
    after = half
    bit = 2 * nz
    while bit < total:
        half = half + exchange(half, bit)
        bit *= 2
    return half, exchange(half, nz), after


def on_device(start_block, diagonal, gaussian, bucket, flip):
    count, ny, nz, width = start_block.shape
    cells = width * ny * lax.axis_size("gy") * nz * lax.axis_size("gz")
    scale = 1.0 / math.sqrt(cells)
    f32, bf16 = jnp.float32, jnp.bfloat16
    size = (ITERS + 1) * count
    small_rows_y = 2 * nz + 8
    small_rows_z = 2 * (ny + 4) + 16
    code, within, across = call(
        small_y, "small_y",
        [((ny, 128), f32, VMEM), ((small_rows_y, width), f32, VMEM), ((small_rows_y, width), f32, VMEM)],
        [VMEM] * 3,
    )(diagonal, bucket, flip)
    dy = swapped("gy", within, across)
    flat = start_block.reshape(count * ny * nz, width)
    side = (3 * nz, count, width)
    (vt,) = call(
        functools.partial(turned, ny=ny, nz=nz), "turned",
        [((ny * nz, count, width), f32, VMEM)],
        [VMEM],
    )(flat)
    codes, within, across = call(
        small_z, "small_z",
        [((16, 128), f32, VMEM), ((small_rows_z, width), f32, VMEM), ((small_rows_z, width), f32, VMEM)],
        [VMEM] * 4,
    )(diagonal, code, *dy)
    dz = swapped("gz", within, across)
    y_halo = swapped(
        "gy",
        *call(
            functools.partial(pack_y, ny=ny, nz=nz), "pack_y",
            [(side, f32, VMEM), (side, f32, VMEM)],
            [VMEM] * 2,
        )(vt, codes),
    )
    half = (BUCKETS // 2 * size, 128)
    field = lambda ring: pltpu.VMEM((ny + 2 * ring, nz + 2 * ring, count, width), f32)
    spread = pltpu.VMEM((ny + 4, nz + 4, 8, width), f32)
    kept, given = call(
        local_sketches, "local_sketches",
        [(half, f32, VMEM), (half, f32, VMEM)],
        [VMEM] * 8,
        [
            field(2), field(3), field(2), spread,
            pltpu.VMEM((32 * BUCKETS, 128), f32), pltpu.SMEM((32 * BUCKETS, 128), f32),
            pltpu.VMEM((BUCKETS, size, width), f32), pltpu.SemaphoreType.DMA,
        ],
        limit=28,
    )(vt, diagonal, codes, *dy, *dz, gaussian)
    kept, got, after = reduced(kept, given)
    z_side = (ny + 6, 3, count, width)
    z_halo = swapped(
        "gz",
        *call(
            functools.partial(pack_z, ny=ny, nz=nz), "pack_z",
            [(z_side, f32, VMEM), (z_side, f32, VMEM)],
            [VMEM] * 4,
        )(vt, *y_halo, after),
    )
    columns = (ny * nz, size, width)
    pair = [pltpu.VMEM(columns, bf16), pltpu.VMEM(columns, bf16)]
    sems = pltpu.SemaphoreType.DMA((2,))
    high, low = call(
        krylov, "krylov",
        [(columns, bf16, HBM), (columns, bf16, HBM)],
        [VMEM] * 10,
        [field(3), field(3), spread, *pair, sems],
        limit=36,
    )(vt, diagonal, *dy, *dz, *y_halo, *z_halo)
    square = (ITERS, count, count)
    basis, alphas, factors = call(
        functools.partial(finish, ny=ny, nz=nz, scale=scale), "finish",
        [(start_block.shape, f32, HBM), (square, f32, VMEM), (square, f32, VMEM)],
        [VMEM, VMEM, HBM, HBM],
        [*pair, pltpu.VMEM((ny, count * nz, width), f32), sems, pltpu.SemaphoreType.DMA],
        limit=28,
    )(kept, got, high, low)
    return basis, alphas, factors


def solution(mesh):
    in_specs = (P(None, "gy", "gz", None), P("gy", "gz", None), P(), P("gy", "gz"), P("gy", "gz"))
    out_specs = (P(None, "gy", "gz", None), P(), P())
    return jax.shard_map(
        on_device, mesh=mesh, in_specs=in_specs, out_specs=out_specs, check_vma=False
    )
```

time: 290 us -> 78.2 us (0.27)
  blocking collectives: 172 us -> 0 us
  matrix products: 51.2 us -> 0 us
  Pallas kernels: 0 us -> 32.9 us
  other arithmetic: 22.3 us -> 0.05 us
  waiting for transfers between devices: 4.42 us -> 25.4 us
  starting transfers between devices: 30.5 us -> 14.9 us
  local copies, waits for them, and re-layouts: 7.46 us -> 3.87 us
    psum x4 -> x0, blocking collectives: 172 us -> none  [total_sketch(): summed = lax.psum(partial_value, ('gy', 'gz'))]
    dot_general x37 -> x0, matrix products: 50.4 us -> none  [the longest x4 17 us: normalize(): basis = jnp.tensordot(inverse, raw, axes=1, precision=HIGH)]
    pallas_call x0 -> x8, Pallas kernels: none -> 32.9 us  [the longest x1 12.2 us: on_device(): call(local_sketches, 'local_sketches', [(half, f32, VMEM), (half, f32, VM...]
    ppermute x12 -> x14, waiting for transfers between devices: 4.42 us -> 25.4 us  [the longest x6 17.1 us: exchange(): return lax.ppermute(value, AXES, [(i, i ^ bit) for i in range(total)])]
    another operation x21 -> x0, other arithmetic: 16.7 us -> none  [the longest x12 8.61 us: normalize(): lower = jnp.linalg.cholesky(gram)]
    ppermute x12 -> x14, starting transfers between devices: 30.5 us -> 14.9 us  [the longest x4 9.97 us: swapped(): lax.ppermute(across, axis, pairs(axis, 1))]
    sub x3 -> x0, other arithmetic: 4.85 us -> none  [apply_operator(): return (6.0 + diagonal) * block - beside]
    unnamed x23 -> x12, local copies, waits for them, and re-layouts: 5.98 us -> 3.87 us
  transfers between devices with their start and end apart: 12 -> 14, of which waited for: 5 -> 7; matrix products, arithmetic and copies ran while one was open for 0% -> 0% of each run, Pallas kernels for 0% -> 29%
where the time goes in v1:
time: 78.2 us; the launch traced here: 78 us
  Pallas kernels  32.9 us (42%)
  waiting for transfers between devices  25.4 us (32%)
  starting transfers between devices  14.9 us (19%)
  local copies, waits for them, and re-layouts  3.87 us (5%)
  between operations  0.81 us (1%)
    ppermute x6, waiting for transfers between devices, exchange(): return lax.ppermute(value, AXES, [(i, i ^ bit) for i in range(total)])  17.1 us
    pallas_call x1, Pallas kernels, on_device(): call(local_sketches, 'local_sketches', [(half, f32, VMEM), (half, f32, VM...  12.2 us
    pallas_call x1, Pallas kernels, on_device(): call(functools.partial(finish, ny=ny, nz=nz, scale=scale), 'finish', [(st...  10.2 us
    ppermute x4, starting transfers between devices, swapped(): lax.ppermute(across, axis, pairs(axis, 1))  9.97 us
    pallas_call x1, Pallas kernels, on_device(): call(krylov, 'krylov', [(columns, bf16, HBM), (columns, bf16, HBM)], [VME...  9.01 us
    ppermute x4, waiting for transfers between devices, swapped(): lax.ppermute(across, axis, pairs(axis, 1))  8.26 us
    unnamed x12, local copies, waits for them, and re-layouts  3.87 us
    ppermute x6, starting transfers between devices, exchange(): return lax.ppermute(value, AXES, [(i, i ^ bit) for i in range(total)])  2.7 us
  transfers between devices with their start and end apart: 14, of which 7 were waited for; matrix products, arithmetic and copies ran while one was open for 0% of the time, Pallas kernels for 29%

profile of v1, /device:TPU:0, one launch (start us, length us, event | category | flops | bytes accessed | tf_op | source)
XLA Modules:
  0.0 78.0 jit_solution(9366656464562206001)
XLA Ops:
  0.6 0.9 %copy-done = f32[8,32,128]{2,1,0:T(8,128)S(1)} copy-done((f32[8,32,128]{2,1,0:T(8,128)S(1)}, f32[8,32,128]{2,1,0:T(8,128)}, u32[]{:S(2)}) %copy-start) | copy-done | bytes 131096
  1.5 0.7 copy-done.4
  2.2 0.7 copy-done.5
  2.9 0.6 collective-permute-start
  3.5 3.5 %collective-permute-start.1 = (f32[72,128]{1,0:T(8,128)S(1)}, f32[72,128]{1,0:T(8,128)S(1)}, u32[]{:S(2)}, u32[]{:S(2)}) collective-permute-start(f32[72,128]{1,0:T(8,128)S(1)} %get-tuple-element.19), channel_id=1, source_target_pairs={{0,28},{4,8},{8,4},{12,16},{16,12},{20,24},{24,20},{28,0},{1,29},{... | collective-permute-start | bytes 110600 | tf_op jit(solution)/shard_map/ppermute | solution.py:46
  7.0 1.6 %copy-done.2 = f32[16,8,32,128]{3,2,1,0:T(8,128)S(1)} copy-done((f32[16,8,32,128]{3,2,1,0:T(8,128)S(1)}, f32[16,8,32,128]{3,2,1,0:T(8,128)}, u32[]{:S(2)}) %copy-start.2) | copy-done | bytes 2097176
  8.6 1.3 %turned.1.vt = f32[256,16,128]{2,1,0:T(8,128)S(1)} custom-call(f32[4096,128]{1,0:T(8,128)S(1)} %bitcast.1), custom_call_target="tpu_custom_call" | custom-call | tf_op jit(solution)/shard_map/turned/pallas_call | solution.py:564
  10.0 0.1 small_z.1
  10.1 0.1 pack_y.1
  10.2 0.1 collective-permute-start.10
  10.3 1.4 %collective-permute-start.11 = (f32[96,16,128]{2,1,0:T(8,128)S(1)}, f32[96,16,128]{2,1,0:T(8,128)S(1)}, u32[]{:S(2)}, u32[]{:S(2)}) collective-permute-start(f32[96,16,128]{2,1,0:T(8,128)S(1)} %get-tuple-element.26), channel_id=1, source_target_pairs={{0,28},{4,8},{8,4},{12,16},{16,12},{20,24},{24,20},{28,0},{1,29},{... | collective-permute-start | bytes 2359304 | tf_op jit(solution)/shard_map/ppermute | solution.py:46
  11.7 1.6 %collective-permute-start.2 = (f32[40,128]{1,0:T(8,128)S(1)}, f32[40,128]{1,0:T(8,128)S(1)}, u32[]{:S(2)}, u32[]{:S(2)}) collective-permute-start(f32[40,128]{1,0:T(8,128)S(1)} %get-tuple-element.21), channel_id=1, source_target_pairs={{0,1},{1,0},{2,3},{3,2},{4,5},{5,4},{6,7},{7,6},{8,9},{9,8},{10,11... | collective-permute-start | bytes 61448 | tf_op jit(solution)/shard_map/ppermute | solution.py:46
  13.2 2.5 %collective-permute-start.3 = (f32[40,128]{1,0:T(8,128)S(1)}, f32[40,128]{1,0:T(8,128)S(1)}, u32[]{:S(2)}, u32[]{:S(2)}) collective-permute-start(f32[40,128]{1,0:T(8,128)S(1)} %get-tuple-element.22), channel_id=1, source_target_pairs={{0,3},{1,2},{2,1},{3,0},{4,7},{5,6},{6,5},{7,4},{8,11},{9,10},{10,... | collective-permute-start | bytes 61448 | tf_op jit(solution)/shard_map/ppermute | solution.py:46
  15.7 3.1 %collective-permute-done.3.z_across.dz_across = f32[40,128]{1,0:T(8,128)S(1)} collective-permute-done((f32[40,128]{1,0:T(8,128)S(1)}, f32[40,128]{1,0:T(8,128)S(1)}, u32[]{:S(2)}, u32[]{:S(2)}) %collective-permute-start.3) | collective-permute-done | bytes 20512 | tf_op jit(solution)/shard_map/ppermute | solution.py:46
  18.8 12.2 %local_sketches.1 = (f32[128,128]{1,0:T(8,128)S(1)}, f32[128,128]{1,0:T(8,128)S(1)}) custom-call(f32[256,16,128]{2,1,0:T(8,128)S(1)} %turned.1.vt, f32[8,32,128]{2,1,0:T(8,128)S(1)} %copy-done.1, f32[16,128]{1,0:T(8,128)S(1)} %get-tuple-element.20.code.after, f32[72,128]{1,0:T(8,128)S(1)} %collective-permute-done.got_within.y_within.dy_within, ...), custom_call_target="tpu_custom_call" | custom-call | tf_op jit(solution)/shard_map/local_sketches/pallas_call | solution.py:586
  31.0 0.1 collective-permute-start.4
  31.1 1.2 %collective-permute-done.4 = f32[128,128]{1,0:T(8,128)S(1)} collective-permute-done((f32[128,128]{1,0:T(8,128)S(1)}, f32[128,128]{1,0:T(8,128)S(1)}, u32[]{:S(2)}, u32[]{:S(2)}) %collective-permute-start.4) | collective-permute-done | bytes 65568 | tf_op jit(solution)/shard_map/ppermute | solution.py:533
  32.3 0.1 collective-permute-start.5
  32.4 4.3 %collective-permute-done.5 = f32[128,128]{1,0:T(8,128)S(1)} collective-permute-done((f32[128,128]{1,0:T(8,128)S(1)}, f32[128,128]{1,0:T(8,128)S(1)}, u32[]{:S(2)}, u32[]{:S(2)}) %collective-permute-start.5) | collective-permute-done | bytes 65568 | tf_op jit(solution)/shard_map/ppermute | solution.py:533
  36.7 1.3 %collective-permute-start.6 = (f32[128,128]{1,0:T(8,128)S(1)}, f32[128,128]{1,0:T(8,128)S(1)}, u32[]{:S(2)}, u32[]{:S(2)}) collective-permute-start(f32[128,128]{1,0:T(8,128)S(1)} %add.16), channel_id=1, source_target_pairs={{0,2},{1,3},{2,0},{3,1},{4,6},{5,7},{6,4},{7,5},{8,10},{9,11},{10,... | collective-permute-start | bytes 196616 | tf_op jit(solution)/shard_map/ppermute | solution.py:533
  37.9 4.3 %collective-permute-done.6 = f32[128,128]{1,0:T(8,128)S(1)} collective-permute-done((f32[128,128]{1,0:T(8,128)S(1)}, f32[128,128]{1,0:T(8,128)S(1)}, u32[]{:S(2)}, u32[]{:S(2)}) %collective-permute-start.6) | collective-permute-done | bytes 65568 | tf_op jit(solution)/shard_map/ppermute | solution.py:533
  42.2 0.1 pack_z.1
  42.3 0.1 collective-permute-start.12
  42.4 2.5 %collective-permute-start.13 = (f32[14,3,16,128]{3,2,1,0:T(8,128)S(1)}, f32[14,3,16,128]{3,2,1,0:T(8,128)S(1)}, u32[]{:S(2)}, u32[]{:S(2)}) collective-permute-start(f32[14,3,16,128]{3,2,1,0:T(8,128)S(1)} %get-tuple-element.28), channel_id=1, source_target_pairs={{0,3},{1,2},{2,1},{3,0},{4,7},{5,6},{6,5},{7,4},{8,11},{9,10},{10,... | collective-permute-start | bytes 1032200 | tf_op jit(solution)/shard_map/ppermute | solution.py:46
  44.9 0.7 collective-permute-start.7
  45.6 3.6 %collective-permute-done.7 = f32[128,128]{1,0:T(8,128)S(1)} collective-permute-done((f32[128,128]{1,0:T(8,128)S(1)}, f32[128,128]{1,0:T(8,128)S(1)}, u32[]{:S(2)}, u32[]{:S(2)}) %collective-permute-start.7) | collective-permute-done | bytes 65568 | tf_op jit(solution)/shard_map/ppermute | solution.py:533
  49.2 0.5 collective-permute-start.8
  49.8 3.8 %collective-permute-done.8 = f32[128,128]{1,0:T(8,128)S(1)} collective-permute-done((f32[128,128]{1,0:T(8,128)S(1)}, f32[128,128]{1,0:T(8,128)S(1)}, u32[]{:S(2)}, u32[]{:S(2)}) %collective-permute-start.8) | collective-permute-done | bytes 65568 | tf_op jit(solution)/shard_map/ppermute | solution.py:533
  53.6 0.1 collective-permute-start.9
  53.6 5.2 %collective-permute-done.13.z_across = f32[14,3,16,128]{3,2,1,0:T(8,128)S(1)} collective-permute-done((f32[14,3,16,128]{3,2,1,0:T(8,128)S(1)}, f32[14,3,16,128]{3,2,1,0:T(8,128)S(1)}, u32[]{:S(2)}, u32[]{:S(2)}) %collective-permute-start.13) | collective-permute-done | bytes 344096 | tf_op jit(solution)/shard_map/ppermute | solution.py:46
  58.8 9.0 %krylov.1 = (bf16[256,64,128]{2,1,0:T(8,128)(2,1)S(1)}, bf16[256,64,128]{2,1,0:T(8,128)(2,1)S(1)}) custom-call(f32[256,16,128]{2,1,0:T(8,128)S(1)} %turned.1.vt, f32[8,32,128]{2,1,0:T(8,128)S(1)} %copy-done.1, f32[72,128]{1,0:T(8,128)S(1)} %collective-permute-done.got_within.y_within.dy_within, ...), custom_call_target="tpu_custom_call" | custom-call | tf_op jit(solution)/shard_map/krylov/pallas_call | solution.py:610
  67.8 10.2 %finish.1 = (f32[16,8,32,128]{3,2,1,0:T(8,128)}, f32[3,16,16]{2,1,0:T(8,128)}, f32[3,16,16]{2,1,0:T(8,128)}) custom-call(f32[128,128]{1,0:T(8,128)S(1)} %add.19.kept, f32[128,128]{1,0:T(8,128)S(1)} %collective-permute-done.9.got, bf16[256,64,128]{2,1,0:T(8,128)(2,1)S(1)} %get-tuple-element.29.high_in, bf16[256,64,128]{2,1,0:T(8,128)(2,1)S(1)} %get-tuple-element.30.low_in), custom_call_target="tpu_custom_call" | custom-call | tf_op jit(solution)/shard_map/finish/pallas_call | solution.py:618
  (21 shorter events, 0.1 us)
Async XLA Ops:
  0.6 0.9 %copy-start = (f32[8,32,128]{2,1,0:T(8,128)S(1)}, f32[8,32,128]{2,1,0:T(8,128)}, u32[]{:S(2)}) copy-start(f32[8,32,128]{2,1,0:T(8,128)} %diag.7) | copy-start | bytes 393220
  1.5 0.7 copy-start.4
  2.2 0.7 copy-start.5
  2.9 7.0 %collective-permute-start = (f32[72,128]{1,0:T(8,128)S(1)}, f32[72,128]{1,0:T(8,128)S(1)}, u32[]{:S(2)}, u32[]{:S(2)}) collective-permute-start(f32[72,128]{1,0:T(8,128)S(1)} %get-tuple-element.18), channel_id=1, source_target_pairs={{0,4},{4,0},{8,12},{12,8},{16,20},{20,16},{24,28},{28,24},{1,5},{5... | collective-permute-start | bytes 110600 | tf_op jit(solution)/shard_map/ppermute | solution.py:46
  3.5 6.5 %collective-permute-start.1 = (f32[72,128]{1,0:T(8,128)S(1)}, f32[72,128]{1,0:T(8,128)S(1)}, u32[]{:S(2)}, u32[]{:S(2)}) collective-permute-start(f32[72,128]{1,0:T(8,128)S(1)} %get-tuple-element.19), channel_id=1, source_target_pairs={{0,28},{4,8},{8,4},{12,16},{16,12},{20,24},{24,20},{28,0},{1,29},{... | collective-permute-start | bytes 110600 | tf_op jit(solution)/shard_map/ppermute | solution.py:46
  7.0 1.6 %copy-start.2 = (f32[16,8,32,128]{3,2,1,0:T(8,128)S(1)}, f32[16,8,32,128]{3,2,1,0:T(8,128)}, u32[]{:S(2)}) copy-start(f32[16,8,32,128]{3,2,1,0:T(8,128)} %param.5) | copy-start | bytes 6291460
  8.6 1.3 %copy-start.1 = (f32[8,32,128]{2,1,0:T(8,128)S(1)}, f32[8,32,128]{2,1,0:T(8,128)}, u32[]{:S(2)}) copy-start(f32[8,32,128]{2,1,0:T(8,128)} %diag.7) | copy-start | bytes 393220
  9.9 8.9 %copy-start.3 = (f32[512,128]{1,0:T(8,128)S(1)}, f32[512,128]{1,0:T(8,128)}, u32[]{:S(2)}) copy-start(f32[512,128]{1,0:T(8,128)} %gaussian.1) | copy-start | bytes 786436
  10.2 32.0 %collective-permute-start.10 = (f32[96,16,128]{2,1,0:T(8,128)S(1)}, f32[96,16,128]{2,1,0:T(8,128)S(1)}, u32[]{:S(2)}, u32[]{:S(2)}) collective-permute-start(f32[96,16,128]{2,1,0:T(8,128)S(1)} %get-tuple-element.25), channel_id=1, source_target_pairs={{0,4},{4,0},{8,12},{12,8},{16,20},{20,16},{24,28},{28,24},{1,5},{5... | collective-permute-start | bytes 2359304 | tf_op jit(solution)/shard_map/ppermute | solution.py:46
  10.3 32.0 %collective-permute-start.11 = (f32[96,16,128]{2,1,0:T(8,128)S(1)}, f32[96,16,128]{2,1,0:T(8,128)S(1)}, u32[]{:S(2)}, u32[]{:S(2)}) collective-permute-start(f32[96,16,128]{2,1,0:T(8,128)S(1)} %get-tuple-element.26), channel_id=1, source_target_pairs={{0,28},{4,8},{8,4},{12,16},{16,12},{20,24},{24,20},{28,0},{1,29},{... | collective-permute-start | bytes 2359304 | tf_op jit(solution)/shard_map/ppermute | solution.py:46
  11.7 4.1 %collective-permute-start.2 = (f32[40,128]{1,0:T(8,128)S(1)}, f32[40,128]{1,0:T(8,128)S(1)}, u32[]{:S(2)}, u32[]{:S(2)}) collective-permute-start(f32[40,128]{1,0:T(8,128)S(1)} %get-tuple-element.21), channel_id=1, source_target_pairs={{0,1},{1,0},{2,3},{3,2},{4,5},{5,4},{6,7},{7,6},{8,9},{9,8},{10,11... | collective-permute-start | bytes 61448 | tf_op jit(solution)/shard_map/ppermute | solution.py:46
  13.2 5.6 %collective-permute-start.3 = (f32[40,128]{1,0:T(8,128)S(1)}, f32[40,128]{1,0:T(8,128)S(1)}, u32[]{:S(2)}, u32[]{:S(2)}) collective-permute-start(f32[40,128]{1,0:T(8,128)S(1)} %get-tuple-element.22), channel_id=1, source_target_pairs={{0,3},{1,2},{2,1},{3,0},{4,7},{5,6},{6,5},{7,4},{8,11},{9,10},{10,... | collective-permute-start | bytes 61448 | tf_op jit(solution)/shard_map/ppermute | solution.py:46
  31.0 1.3 %collective-permute-start.4 = (f32[128,128]{1,0:T(8,128)S(1)}, f32[128,128]{1,0:T(8,128)S(1)}, u32[]{:S(2)}, u32[]{:S(2)}) collective-permute-start(f32[128,128]{1,0:T(8,128)S(1)} %get-tuple-element.24), channel_id=1, source_target_pairs={{0,4},{1,5},{2,6},{3,7},{4,0},{5,1},{6,2},{7,3},{8,12},{9,13},{10,... | collective-permute-start | bytes 196616 | tf_op jit(solution)/shard_map/ppermute | solution.py:533
  32.3 4.3 %collective-permute-start.5 = (f32[128,128]{1,0:T(8,128)S(1)}, f32[128,128]{1,0:T(8,128)S(1)}, u32[]{:S(2)}, u32[]{:S(2)}) collective-permute-start(f32[128,128]{1,0:T(8,128)S(1)} %add.15), channel_id=1, source_target_pairs={{0,1},{1,0},{2,3},{3,2},{4,5},{5,4},{6,7},{7,6},{8,9},{9,8},{10,11... | collective-permute-start | bytes 196616 | tf_op jit(solution)/shard_map/ppermute | solution.py:533
  36.7 5.5 %collective-permute-start.6 = (f32[128,128]{1,0:T(8,128)S(1)}, f32[128,128]{1,0:T(8,128)S(1)}, u32[]{:S(2)}, u32[]{:S(2)}) collective-permute-start(f32[128,128]{1,0:T(8,128)S(1)} %add.16), channel_id=1, source_target_pairs={{0,2},{1,3},{2,0},{3,1},{4,6},{5,7},{6,4},{7,5},{8,10},{9,11},{10,... | collective-permute-start | bytes 196616 | tf_op jit(solution)/shard_map/ppermute | solution.py:533
  42.3 11.3 %collective-permute-start.12 = (f32[14,3,16,128]{3,2,1,0:T(8,128)S(1)}, f32[14,3,16,128]{3,2,1,0:T(8,128)S(1)}, u32[]{:S(2)}, u32[]{:S(2)}) collective-permute-start(f32[14,3,16,128]{3,2,1,0:T(8,128)S(1)} %get-tuple-element.27), channel_id=1, source_target_pairs={{0,1},{1,0},{2,3},{3,2},{4,5},{5,4},{6,7},{7,6},{8,9},{9,8},{10,11... | collective-permute-start | bytes 1032200 | tf_op jit(solution)/shard_map/ppermute | solution.py:46
  42.4 16.4 %collective-permute-start.13 = (f32[14,3,16,128]{3,2,1,0:T(8,128)S(1)}, f32[14,3,16,128]{3,2,1,0:T(8,128)S(1)}, u32[]{:S(2)}, u32[]{:S(2)}) collective-permute-start(f32[14,3,16,128]{3,2,1,0:T(8,128)S(1)} %get-tuple-element.28), channel_id=1, source_target_pairs={{0,3},{1,2},{2,1},{3,0},{4,7},{5,6},{6,5},{7,4},{8,11},{9,10},{10,... | collective-permute-start | bytes 1032200 | tf_op jit(solution)/shard_map/ppermute | solution.py:46
  44.9 4.3 %collective-permute-start.7 = (f32[128,128]{1,0:T(8,128)S(1)}, f32[128,128]{1,0:T(8,128)S(1)}, u32[]{:S(2)}, u32[]{:S(2)}) collective-permute-start(f32[128,128]{1,0:T(8,128)S(1)} %add.17.after), channel_id=1, source_target_pairs={{0,8},{1,9},{2,10},{3,11},{4,12},{5,13},{6,14},{7,15},{8,0},{9,1},... | collective-permute-start | bytes 196616 | tf_op jit(solution)/shard_map/ppermute | solution.py:533
  49.2 4.3 %collective-permute-start.8 = (f32[128,128]{1,0:T(8,128)S(1)}, f32[128,128]{1,0:T(8,128)S(1)}, u32[]{:S(2)}, u32[]{:S(2)}) collective-permute-start(f32[128,128]{1,0:T(8,128)S(1)} %add.18), channel_id=1, source_target_pairs={{0,16},{1,17},{2,18},{3,19},{4,20},{5,21},{6,22},{7,23},{8,24},{9,... | collective-permute-start | bytes 196616 | tf_op jit(solution)/shard_map/ppermute | solution.py:533
  53.6 14.3 %collective-permute-start.9 = (f32[128,128]{1,0:T(8,128)S(1)}, f32[128,128]{1,0:T(8,128)S(1)}, u32[]{:S(2)}, u32[]{:S(2)}) collective-permute-start(f32[128,128]{1,0:T(8,128)S(1)} %add.19.kept), channel_id=1, source_target_pairs={{0,4},{1,5},{2,6},{3,7},{4,0},{5,1},{6,2},{7,3},{8,12},{9,13},{10,... | collective-permute-start | bytes 196616 | tf_op jit(solution)/shard_map/ppermute | solution.py:533
